TPU v7x, 32 devices: a whole 2x2x4 slice. The times are simulated.
32 devices in a mesh: section: 4 (over y, x), cp: 4 (over z), tp: 2 (over core).
Axes of the slice: x: 2, y: 2, z: 4, core: 2. Of those that a mesh axis runs over, the one named last changes fastest.
Arguments:
- acts: bfloat16 [4, 512, 8192], P('section', 'cp', 'tp'), may hold values from -16 to 16
- keys: bfloat16 [4, 512, 1024], P('section', 'cp', 'tp'), may hold values from -4 to 4
- values: bfloat16 [4, 512, 1024], P('section', 'cp', 'tp'), may hold values from -6 to 6
- grads: bfloat16 [4, 512, 8192], P('section', 'cp', 'tp'), may hold values from -6 to 6
- docs: int32 [4, 512], P('section'), may hold values from 0 to 7, never falling along the last dimension, each value on 1 to 256 neighbouring positions
- order: int32 [4, 512], P('section'), may hold values from 0 to 511, each once within a row
Outputs:
- outputs: bfloat16 [4, 512, 8192], P('section', 'cp', 'tp')
- grad_query: bfloat16 [4, 512, 8192], P('section', 'cp', 'tp')
- grad_keys: bfloat16 [4, 512, 1024], P('section', 'cp', 'tp')
- grad_values: bfloat16 [4, 512, 1024], P('section', 'cp', 'tp')
Inputs may be any that keep to these rules, and one draw needn't show every extreme that they name: `docs`: along positions of one section the document numbers never fall; each document holds 1 to 256 tokens. `order`: each section's row holds every position once.
All inputs are finite; a program needn't handle non-finite values.
Results may differ from a plain program's by a relative error of at most 0.0061.
Values may be sent and summed in bfloat16 or wider, within the bound.
A program may use at most 64 MiB of HBM per device.

v0:
```python
import functools

import jax
import jax.numpy as jnp
from jax import lax
from jax.experimental import pallas as pl
from jax.experimental.pallas import tpu as pltpu
from jax.sharding import PartitionSpec as P

HEAD = 128
DOCS = 8
MESH = pl.DeviceIdType.MESH


def times(a, b, dims):
    return lax.dot_general(a, b, (dims, ((), ())), preferred_element_type=jnp.float32)


def relay_kernel(
    heads, packs, pack, sections, blocks,
    acts, keys, values, grads, docs, order,
    out, gq, gk, gv,
    qbuf, gbuf, kbuf, vbuf, kt, vt, bias, dk, dv, terms, met,
    sec_send, sec_recv, kv_send, kv_recv, own_sem, red_send, red_recv,
):
    scale = HEAD ** (-0.5)
    tok = qbuf.shape[1]
    wide_cols = pack * HEAD
    section = lax.axis_index("section")
    me = lax.axis_index("cp")
    after = lax.rem(section + 1, sections)
    before = lax.rem(section + sections - 1, sections)

    def peer(off):
        return lax.rem(me + off, blocks)

    barrier = pltpu.get_barrier_semaphore()
    for where in (after, before):
        pl.semaphore_signal(barrier, inc=1, device_id={"section": where}, device_id_type=MESH)
    for off in range(1, blocks):
        pl.semaphore_signal(barrier, inc=1, device_id={"cp": peer(off)}, device_id_type=MESH)
    pl.semaphore_wait(barrier, 1 + blocks)

    def moved(step, which):
        src, dst, where = ((acts, qbuf, after), (grads, gbuf, before))[which]
        cols = pl.ds(pl.multiple_of(step * wide_cols, wide_cols), wide_cols)
        return pltpu.make_async_remote_copy(
            src_ref=src.at[0, :, cols],
            dst_ref=dst.at[step],
            send_sem=sec_send.at[step, which],
            recv_sem=sec_recv.at[step, which],
            device_id={"section": where},
            device_id_type=MESH,
        )

    def mine(ref, head):
        cols = pl.ds(pl.multiple_of(head * HEAD, HEAD), HEAD)
        return ref.at[0, :, cols]

    own_rows = pl.ds(pl.multiple_of(me * tok, tok), tok)

    def shared(head, which, off):
        src, dst = ((keys, kbuf), (values, vbuf))[which]
        return pltpu.make_async_remote_copy(
            src_ref=mine(src, head),
            dst_ref=dst.at[head, own_rows],
            send_sem=kv_send.at[head, which, off - 1],
            recv_sem=kv_recv.at[head, which, off - 1],
            device_id={"cp": peer(off)},
            device_id_type=MESH,
        )

    def kept(head, which):
        src, dst = ((keys, kbuf), (values, vbuf))[which]
        return pltpu.make_async_copy(
            mine(src, head), dst.at[head, own_rows], own_sem.at[head, which]
        )

    def returned(head, off):
        rows = pl.ds(pl.multiple_of(peer(off) * tok, tok), tok)
        return pltpu.make_async_remote_copy(
            src_ref=terms.at[head, rows],
            dst_ref=met.at[head, off - 1],
            send_sem=red_send.at[head, off - 1],
            recv_sem=red_recv.at[head, off - 1],
            device_id={"cp": peer(off)},
            device_id_type=MESH,
        )

    @pl.loop(0, heads)
    def _(head):
        @pl.loop(0, packs)
        def _(p):
            for which in range(2):
                moved(head * packs + p, which).start()

        for which in range(2):
            for off in range(1, blocks):
                shared(head, which, off).start()
            kept(head, which).start()

    positions = order[...].astype(jnp.float32)
    asked = order[:, own_rows].astype(jnp.float32)
    low = jnp.zeros_like(asked)
    for doc in range(1, DOCS):
        start = jnp.sum(
            jnp.where(docs[...] < doc, 1.0, 0.0), axis=1, keepdims=True
        )
        low = jnp.maximum(low, jnp.where(start <= asked, start, 0.0))
    count = positions.shape[1]
    stored = jnp.broadcast_to(positions, (tok, count)).T
    allowed = (stored <= asked) & (stored >= low)
    bias[...] = jnp.where(allowed, 0.0, -1e30)

    def finish(head):
        total = terms[head, own_rows, :].astype(jnp.float32)
        for off in range(1, blocks):
            returned(head, off).wait_recv()
            total = total + met[head, off - 1].astype(jnp.float32)
        cols = pl.ds(pl.multiple_of(head * HEAD, HEAD), HEAD)
        gk[0, :, cols] = total[:, :HEAD].astype(jnp.bfloat16)
        gv[0, :, cols] = total[:, HEAD:].astype(jnp.bfloat16)

    @pl.loop(0, heads)
    def _(head):
        for which in range(2):
            kept(head, which).wait()
            for off in range(1, blocks):
                shared(head, which, off).wait_recv()
        kt[...] = kbuf[head].T
        vt[...] = vbuf[head].T
        dk[...] = jnp.zeros_like(dk)
        dv[...] = jnp.zeros_like(dv)

        @pl.loop(0, packs)
        def _(p):
            step = head * packs + p
            for which in range(2):
                moved(step, which).wait_recv()
            parts = [slice(j * HEAD, (j + 1) * HEAD) for j in range(pack)]
            q = jnp.concatenate([qbuf[step, :, c] for c in parts], axis=0)
            g = jnp.concatenate([gbuf[step, :, c] for c in parts], axis=0)
            masked = jnp.concatenate([bias[...]] * pack, axis=1)
            k, v = kbuf[head], vbuf[head]
            scores = times(k, q, ((1,), (1,))) * scale + masked
            expd = jnp.exp(scores - jnp.max(scores, axis=0, keepdims=True))
            probs = (expd * (1.0 / jnp.sum(expd, axis=0, keepdims=True))).astype(jnp.bfloat16)
            attended = times(vt[...], probs, ((1,), (0,))).T
            dprob = times(v, g, ((1,), (1,)))
            wide = probs.astype(jnp.float32)
            delta = jnp.sum(wide * dprob, axis=0, keepdims=True)
            dscore = (wide * (dprob - delta)).astype(jnp.bfloat16)
            dquery = times(kt[...], dscore, ((1,), (0,))).T
            full = (q.astype(jnp.float32) + attended).astype(jnp.bfloat16)
            grad = (g.astype(jnp.float32) + dquery * scale).astype(jnp.bfloat16)
            for j in range(pack):
                cols = pl.ds(pl.multiple_of(step * wide_cols + j * HEAD, HEAD), HEAD)
                out[0, :, cols] = full[j * tok : (j + 1) * tok]
                gq[0, :, cols] = grad[j * tok : (j + 1) * tok]
            dk[...] += times(dscore, q, ((1,), (0,)))
            dv[...] += times(probs, g, ((1,), (0,)))

        terms[head, :, :HEAD] = (dk[...] * scale).astype(jnp.bfloat16)
        terms[head, :, HEAD:] = dv[...].astype(jnp.bfloat16)
        for off in range(1, blocks):
            returned(head, off).start()

        @pl.when(head > 0)
        def _():
            finish(head - 1)

    finish(heads - 1)

    @pl.loop(0, heads)
    def _(head):
        @pl.loop(0, packs)
        def _(p):
            for which in range(2):
                moved(head * packs + p, which).wait_send()

        for off in range(1, blocks):
            for which in range(2):
                shared(head, which, off).wait_send()
            returned(head, off).wait_send()


def on_device(acts, keys, values, grads, docs, order):
    tok = acts.shape[1]
    heads = keys.shape[2] // HEAD
    group = acts.shape[2] // keys.shape[2]
    pack = 2 if group % 2 == 0 else 1
    packs = group // pack
    sections, blocks = lax.axis_size("section"), lax.axis_size("cp")
    count = blocks * tok
    steps = heads * packs
    pairs = group * heads * tok * count
    half, dma = jnp.bfloat16, pltpu.SemaphoreType.DMA
    far = pl.BlockSpec(memory_space=pl.ANY)
    near = pl.BlockSpec(memory_space=pltpu.VMEM)
    return pl.pallas_call(
        functools.partial(relay_kernel, heads, packs, pack, sections, blocks),
        out_shape=(
            jax.ShapeDtypeStruct(acts.shape, half),
            jax.ShapeDtypeStruct(acts.shape, half),
            jax.ShapeDtypeStruct(keys.shape, half),
            jax.ShapeDtypeStruct(keys.shape, half),
        ),
        in_specs=[far] * 4 + [near] * 2,
        out_specs=(near,) * 4,
        scratch_shapes=[
            pltpu.VMEM((steps, tok, pack * HEAD), half),
            pltpu.VMEM((steps, tok, pack * HEAD), half),
            pltpu.VMEM((heads, count, HEAD), half),
            pltpu.VMEM((heads, count, HEAD), half),
            pltpu.VMEM((HEAD, count), half),
            pltpu.VMEM((HEAD, count), half),
            pltpu.VMEM((count, tok), jnp.float32),
            pltpu.VMEM((count, HEAD), jnp.float32),
            pltpu.VMEM((count, HEAD), jnp.float32),
            pltpu.VMEM((heads, count, 2 * HEAD), half),
            pltpu.VMEM((heads, blocks - 1, tok, 2 * HEAD), half),
            dma((steps, 2)),
            dma((steps, 2)),
            dma((heads, 2, blocks - 1)),
            dma((heads, 2, blocks - 1)),
            dma((heads, 2)),
            dma((heads, blocks - 1)),
            dma((heads, blocks - 1)),
        ],
        compiler_params=pltpu.CompilerParams(
            collective_id=0,
            has_side_effects=True,
            vmem_limit_bytes=48 * 1024 * 1024,
        ),
        cost_estimate=pl.CostEstimate(
            flops=12 * HEAD * pairs,
            bytes_accessed=8 * acts.size + 8 * keys.size,
            transcendentals=pairs,
        ),
    )(acts, keys, values, grads, docs, order)


def solution(mesh):
    rows = P("section", "cp", "tp")
    return jax.shard_map(
        on_device,
        mesh=mesh,
        in_specs=(rows, rows, rows, rows, P("section", None), P("section", None)),
        out_specs=(rows, rows, rows, rows),
        check_vma=False,
    )
```

profile of v0, /device:TPU:0, one launch (start us, length us, event | category | flops | bytes accessed | tf_op | source)
XLA Modules:
  0.0 69.2 jit_solution(13848727634140888775)
XLA Ops:
  0.6 0.0 copy-start
  0.6 1.2 %copy-done = bf16[1,128,4096]{2,1,0:T(8,128)(2,1)S(1)} copy-done((bf16[1,128,4096]{2,1,0:T(8,128)(2,1)S(1)}, bf16[1,128,4096]{2,1,0:T(8,128)(2,1)}, u32[]{:S(2)}) %copy-start) | copy-done | bytes 1048600
  1.9 0.0 copy-start.1
  1.9 1.2 %copy-done.1 = bf16[1,128,4096]{2,1,0:T(8,128)(2,1)S(1)} copy-done((bf16[1,128,4096]{2,1,0:T(8,128)(2,1)S(1)}, bf16[1,128,4096]{2,1,0:T(8,128)(2,1)}, u32[]{:S(2)}) %copy-start.1) | copy-done | bytes 1048600
  3.1 0.0 copy-start.2
  3.1 0.9 %copy-done.2 = bf16[1,128,512]{2,1,0:T(8,128)(2,1)S(1)} copy-done((bf16[1,128,512]{2,1,0:T(8,128)(2,1)S(1)}, bf16[1,128,512]{2,1,0:T(8,128)(2,1)}, u32[]{:S(2)}) %copy-start.2) | copy-done | bytes 131096
  4.0 0.0 copy-start.3
  4.0 0.9 %copy-done.3 = bf16[1,128,512]{2,1,0:T(8,128)(2,1)S(1)} copy-done((bf16[1,128,512]{2,1,0:T(8,128)(2,1)S(1)}, bf16[1,128,512]{2,1,0:T(8,128)(2,1)}, u32[]{:S(2)}) %copy-start.3) | copy-done | bytes 131096
  4.9 0.0 copy-start.4
  4.9 0.7 copy-done.4
  5.6 0.0 copy-start.5
  5.6 0.7 copy-done.5
  6.3 59.7 %shard_map.93 = (bf16[1,128,4096]{2,1,0:T(8,128)(2,1)S(1)}, bf16[1,128,4096]{2,1,0:T(8,128)(2,1)S(1)}, bf16[1,128,512]{2,1,0:T(8,128)(2,1)S(1)}, bf16[1,128,512]{2,1,0:T(8,128)(2,1)S(1)}) custom-call(bf16[1,128,4096]{2,1,0:T(8,128)(2,1)S(1)} %copy-done, bf16[1,128,512]{2,1,0:T(8,128)(2,1)S(1)} %copy-done.2, bf16[1,128,512]{2,1,0:T(8,128)(2,1)S(1)} %copy-done.3, ...), custom_call_target="tpu_custom_call" | custom-call | flops 3221225472 | bytes 4718592 | tf_op jit(solution)/shard_map/pallas_call | solution.py:200
  66.0 1.0 %copy.14 = bf16[1,128,4096]{2,1,0:T(8,128)(2,1)} copy(bf16[1,128,4096]{2,1,0:T(8,128)(2,1)S(1)} %get-tuple-element.8) | data formatting | bytes 2097152
  67.0 1.0 %copy.15 = bf16[1,128,4096]{2,1,0:T(8,128)(2,1)} copy(bf16[1,128,4096]{2,1,0:T(8,128)(2,1)S(1)} %get-tuple-element.9) | data formatting | bytes 2097152
  67.9 0.7 copy.16
  68.6 0.7 copy.17
Async XLA Ops:
  0.6 1.2 %copy-start = (bf16[1,128,4096]{2,1,0:T(8,128)(2,1)S(1)}, bf16[1,128,4096]{2,1,0:T(8,128)(2,1)}, u32[]{:S(2)}) copy-start(bf16[1,128,4096]{2,1,0:T(8,128)(2,1)} %acts.1) | copy-start | bytes 3145732
  1.9 1.2 %copy-start.1 = (bf16[1,128,4096]{2,1,0:T(8,128)(2,1)S(1)}, bf16[1,128,4096]{2,1,0:T(8,128)(2,1)}, u32[]{:S(2)}) copy-start(bf16[1,128,4096]{2,1,0:T(8,128)(2,1)} %grads.1) | copy-start | bytes 3145732
  3.1 0.9 %copy-start.2 = (bf16[1,128,512]{2,1,0:T(8,128)(2,1)S(1)}, bf16[1,128,512]{2,1,0:T(8,128)(2,1)}, u32[]{:S(2)}) copy-start(bf16[1,128,512]{2,1,0:T(8,128)(2,1)} %keys.1) | copy-start | bytes 393220
  4.0 0.9 %copy-start.3 = (bf16[1,128,512]{2,1,0:T(8,128)(2,1)S(1)}, bf16[1,128,512]{2,1,0:T(8,128)(2,1)}, u32[]{:S(2)}) copy-start(bf16[1,128,512]{2,1,0:T(8,128)(2,1)} %values.1) | copy-start | bytes 393220
  4.9 0.7 copy-start.4
  5.6 0.7 copy-start.5
where the time goes:
time: 69.5 us; the launch traced here: 69.2 us
  Pallas kernels  59.7 us (86%)
  local copies, waits for them, and re-layouts  8.86 us (13%)
    pallas_call x1, Pallas kernels, on_device(): pl.pallas_call(functools.partial(relay_kernel, heads, packs, pack, sectio...  59.7 us
    unnamed x16, local copies, waits for them, and re-layouts  8.86 us

commit v1 on v0

--- a/solution.py
+++ b/solution.py
@@ -20,8 +20,8 @@
     heads, packs, pack, sections, blocks,
     acts, keys, values, grads, docs, order,
     out, gq, gk, gv,
-    qbuf, gbuf, kbuf, vbuf, kt, vt, bias, dk, dv, terms, met,
-    sec_send, sec_recv, kv_send, kv_recv, own_sem, red_send, red_recv,
+    qbuf, gbuf, kbuf, vbuf, kt, vt, bias, dk, dv, terms, met, held, where_row, doc_row,
+    sec_send, sec_recv, kv_send, kv_recv, own_sem, red_send, red_recv, row_sem, token,
 ):
     scale = HEAD ** (-0.5)
     tok = qbuf.shape[1]
@@ -31,15 +31,31 @@
     after = lax.rem(section + 1, sections)
     before = lax.rem(section + sections - 1, sections)
 
+    middle = blocks // 2
+    offs = sorted(range(1, blocks), key=lambda off: abs(off - middle))
+
     def peer(off):
         return lax.rem(me + off, blocks)
 
+    rows = (
+        pltpu.make_async_copy(order, where_row, row_sem.at[0]),
+        pltpu.make_async_copy(docs, doc_row, row_sem.at[1]),
+    )
+    for row in rows:
+        row.start()
     barrier = pltpu.get_barrier_semaphore()
     for where in (after, before):
         pl.semaphore_signal(barrier, inc=1, device_id={"section": where}, device_id_type=MESH)
-    for off in range(1, blocks):
-        pl.semaphore_signal(barrier, inc=1, device_id={"cp": peer(off)}, device_id_type=MESH)
-    pl.semaphore_wait(barrier, 1 + blocks)
+
+    @pl.when(me > 0)
+    def _():
+        pl.semaphore_signal(barrier, inc=1, device_id={"cp": me - 1}, device_id_type=MESH)
+
+    @pl.when(me < blocks - 1)
+    def _():
+        pl.semaphore_signal(barrier, inc=1, device_id={"cp": me + 1}, device_id_type=MESH)
+
+    pl.semaphore_wait(barrier, 2 + (me + blocks - 1) // blocks + (2 * blocks - 2 - me) // blocks)
 
     def moved(step, which):
         src, dst, where = ((acts, qbuf, after), (grads, gbuf, before))[which]
@@ -87,24 +103,41 @@
             device_id_type=MESH,
         )
 
+    steps = heads * packs
+
+    @pl.loop(0, steps)
+    def _(step):
+        for which in range(2):
+            moved(step, which).start()
+
+    for side, ahead, behind in ((0, me > 0, me < blocks - 1), (1, me < blocks - 1, me > 0)):
+        step_on = me + 1 - 2 * side
+
+        @pl.when(ahead)
+        def _():
+            pl.semaphore_wait(token.at[side], 1)
+
+        @pl.when(behind)
+        def _():
+            pl.semaphore_signal(
+                token.at[side], inc=1, device_id={"cp": step_on}, device_id_type=MESH
+            )
+
     @pl.loop(0, heads)
     def _(head):
-        @pl.loop(0, packs)
-        def _(p):
-            for which in range(2):
-                moved(head * packs + p, which).start()
-
         for which in range(2):
             for off in range(1, blocks):
                 shared(head, which, off).start()
             kept(head, which).start()
 
-    positions = order[...].astype(jnp.float32)
-    asked = order[:, own_rows].astype(jnp.float32)
+    for row in rows:
+        row.wait()
+    positions = where_row[...].astype(jnp.float32)
+    asked = where_row[:, own_rows].astype(jnp.float32)
     low = jnp.zeros_like(asked)
     for doc in range(1, DOCS):
         start = jnp.sum(
-            jnp.where(docs[...] < doc, 1.0, 0.0), axis=1, keepdims=True
+            jnp.where(doc_row[...] < doc, 1.0, 0.0), axis=1, keepdims=True
         )
         low = jnp.maximum(low, jnp.where(start <= asked, start, 0.0))
     count = positions.shape[1]
@@ -132,56 +165,82 @@
         dk[...] = jnp.zeros_like(dk)
         dv[...] = jnp.zeros_like(dv)
 
-        @pl.loop(0, packs)
-        def _(p):
-            step = head * packs + p
+        def one(step, last):
             for which in range(2):
                 moved(step, which).wait_recv()
+
             parts = [slice(j * HEAD, (j + 1) * HEAD) for j in range(pack)]
             q = jnp.concatenate([qbuf[step, :, c] for c in parts], axis=0)
             g = jnp.concatenate([gbuf[step, :, c] for c in parts], axis=0)
             masked = jnp.concatenate([bias[...]] * pack, axis=1)
-            k, v = kbuf[head], vbuf[head]
-            scores = times(k, q, ((1,), (1,))) * scale + masked
+            scores = times(kbuf[head], q, ((1,), (1,))) * scale + masked
             expd = jnp.exp(scores - jnp.max(scores, axis=0, keepdims=True))
             probs = (expd * (1.0 / jnp.sum(expd, axis=0, keepdims=True))).astype(jnp.bfloat16)
-            attended = times(vt[...], probs, ((1,), (0,))).T
-            dprob = times(v, g, ((1,), (1,)))
+            dprob = times(vbuf[head], g, ((1,), (1,)))
             wide = probs.astype(jnp.float32)
             delta = jnp.sum(wide * dprob, axis=0, keepdims=True)
             dscore = (wide * (dprob - delta)).astype(jnp.bfloat16)
-            dquery = times(kt[...], dscore, ((1,), (0,))).T
-            full = (q.astype(jnp.float32) + attended).astype(jnp.bfloat16)
-            grad = (g.astype(jnp.float32) + dquery * scale).astype(jnp.bfloat16)
+            dv_now = dv[...] + times(probs, g, ((1,), (0,)))
+            dk_now = dk[...] + times(dscore, q, ((1,), (0,)))
             for j in range(pack):
+                held[0, j] = probs[:, j * tok : (j + 1) * tok]
+                held[1, j] = dscore[:, j * tok : (j + 1) * tok]
+            if last:
+                terms[head, :, HEAD:] = dv_now.astype(jnp.bfloat16)
+                terms[head, :, :HEAD] = (dk_now * scale).astype(jnp.bfloat16)
+                for off in offs:
+                    returned(head, off).start()
+            else:
+                dv[...] = dv_now
+                dk[...] = dk_now
+
+            @pl.loop(0, pack)
+            def _(j):
+                attended = times(vt[...], held[0, j], ((1,), (0,))).T
+                dquery = times(kt[...], held[1, j], ((1,), (0,))).T
+                here = pl.ds(pl.multiple_of(j * HEAD, HEAD), HEAD)
                 cols = pl.ds(pl.multiple_of(step * wide_cols + j * HEAD, HEAD), HEAD)
-                out[0, :, cols] = full[j * tok : (j + 1) * tok]
-                gq[0, :, cols] = grad[j * tok : (j + 1) * tok]
-            dk[...] += times(dscore, q, ((1,), (0,)))
-            dv[...] += times(probs, g, ((1,), (0,)))
-
-        terms[head, :, :HEAD] = (dk[...] * scale).astype(jnp.bfloat16)
-        terms[head, :, HEAD:] = dv[...].astype(jnp.bfloat16)
-        for off in range(1, blocks):
-            returned(head, off).start()
+                query = qbuf[step, :, here].astype(jnp.float32)
+                cotan = gbuf[step, :, here].astype(jnp.float32)
+                out[0, :, cols] = (query + attended).astype(jnp.bfloat16)
+                gq[0, :, cols] = (cotan + dquery * scale).astype(jnp.bfloat16)
+
+        @pl.loop(0, packs - 1)
+        def _(p):
+            one(head * packs + p, False)
+
+        one(head * packs + packs - 1, True)
 
         @pl.when(head > 0)
         def _():
             finish(head - 1)
 
-    finish(heads - 1)
+    @pl.loop(0, steps)
+    def _(step):
+        for which in range(2):
+            moved(step, which).wait_send()
 
     @pl.loop(0, heads)
     def _(head):
-        @pl.loop(0, packs)
-        def _(p):
-            for which in range(2):
-                moved(head * packs + p, which).wait_send()
-
         for off in range(1, blocks):
             for which in range(2):
                 shared(head, which, off).wait_send()
+
+    finish(heads - 1)
+
+    @pl.loop(0, heads)
+    def _(head):
+        for off in range(1, blocks):
             returned(head, off).wait_send()
+
+
+def flush_kernel(*refs):
+    sem = refs[-1]
+    copies = [pltpu.make_async_copy(refs[i], refs[4 + i], sem.at[i]) for i in range(4)]
+    for copy in copies:
+        copy.start()
+    for copy in copies:
+        copy.wait()
 
 
 def on_device(acts, keys, values, grads, docs, order):
@@ -195,17 +254,14 @@
     steps = heads * packs
     pairs = group * heads * tok * count
     half, dma = jnp.bfloat16, pltpu.SemaphoreType.DMA
-    far = pl.BlockSpec(memory_space=pl.ANY)
+    far = pl.BlockSpec(memory_space=pltpu.HBM)
     near = pl.BlockSpec(memory_space=pltpu.VMEM)
-    return pl.pallas_call(
+    shapes = tuple(jax.ShapeDtypeStruct(a.shape, half) for a in (acts, acts, keys, keys))
+    args = (acts, keys, values, grads, docs, order)
+    near_results = pl.pallas_call(
         functools.partial(relay_kernel, heads, packs, pack, sections, blocks),
-        out_shape=(
-            jax.ShapeDtypeStruct(acts.shape, half),
-            jax.ShapeDtypeStruct(acts.shape, half),
-            jax.ShapeDtypeStruct(keys.shape, half),
-            jax.ShapeDtypeStruct(keys.shape, half),
-        ),
-        in_specs=[far] * 4 + [near] * 2,
+        out_shape=shapes,
+        in_specs=[far] * 6,
         out_specs=(near,) * 4,
         scratch_shapes=[
             pltpu.VMEM((steps, tok, pack * HEAD), half),
@@ -219,6 +275,9 @@
             pltpu.VMEM((count, HEAD), jnp.float32),
             pltpu.VMEM((heads, count, 2 * HEAD), half),
             pltpu.VMEM((heads, blocks - 1, tok, 2 * HEAD), half),
+            pltpu.VMEM((2, pack, count, tok), half),
+            pltpu.VMEM(order.shape, order.dtype),
+            pltpu.VMEM(docs.shape, docs.dtype),
             dma((steps, 2)),
             dma((steps, 2)),
             dma((heads, 2, blocks - 1)),
@@ -226,6 +285,8 @@
             dma((heads, 2)),
             dma((heads, blocks - 1)),
             dma((heads, blocks - 1)),
+            dma((2,)),
+            pltpu.SemaphoreType.REGULAR((2,)),
         ],
         compiler_params=pltpu.CompilerParams(
             collective_id=0,
@@ -237,7 +298,15 @@
             bytes_accessed=8 * acts.size + 8 * keys.size,
             transcendentals=pairs,
         ),
-    )(acts, keys, values, grads, docs, order)
+    )(*(pltpu.with_memory_space_constraint(arg, pltpu.HBM) for arg in args))
+    return pl.pallas_call(
+        flush_kernel,
+        out_shape=shapes,
+        in_specs=[near] * 4,
+        out_specs=(far,) * 4,
+        scratch_shapes=[dma((4,))],
+        compiler_params=pltpu.CompilerParams(vmem_limit_bytes=8 * 1024 * 1024),
+    )(*near_results)
 
 
 def solution(mesh):

time: 69.5 us -> 61.7 us (0.89)
  local copies, waits for them, and re-layouts: 8.86 us -> 0 us
  Pallas kernels: 59.7 us -> 60.8 us
    unnamed x16 -> x0, local copies, waits for them, and re-layouts: 8.86 us -> none
    pallas_call x0 -> x1, Pallas kernels: none -> 1.43 us  [on_device(): pl.pallas_call(flush_kernel, out_shape=shapes, in_specs=[near] * 4, out_s...]
where the time goes in v1:
time: 61.7 us; the launch traced here: 61.5 us
  Pallas kernels  60.8 us (99%)
  between operations  0.64 us (1%)
    pallas_call x1, Pallas kernels, on_device(): pl.pallas_call(functools.partial(relay_kernel, heads, packs, pack, sectio...  59.4 us
    pallas_call x1, Pallas kernels, on_device(): pl.pallas_call(flush_kernel, out_shape=shapes, in_specs=[near] * 4, out_s...  1.43 us

profile of v1, /device:TPU:0, one launch (start us, length us, event | category | flops | bytes accessed | tf_op | source)
XLA Modules:
  0.0 61.5 jit_solution(13293184414561562738)
XLA Ops:
  0.6 59.4 %shard_map.93 = (bf16[1,128,4096]{2,1,0:T(8,128)(2,1)S(1)}, bf16[1,128,4096]{2,1,0:T(8,128)(2,1)S(1)}, bf16[1,128,512]{2,1,0:T(8,128)(2,1)S(1)}, bf16[1,128,512]{2,1,0:T(8,128)(2,1)S(1)}) custom-call(bf16[1,128,4096]{2,1,0:T(8,128)(2,1)} %acts.1, bf16[1,128,512]{2,1,0:T(8,128)(2,1)} %keys.1, bf16[1,128,512]{2,1,0:T(8,128)(2,1)} %values.1, ...), custom_call_target="tpu_custom_call" | custom-call | flops 3221225472 | bytes 4718592 | tf_op jit(solution)/shard_map/pallas_call | solution.py:261
  60.0 1.4 %shard_map.94 = (bf16[1,128,4096]{2,1,0:T(8,128)(2,1)}, bf16[1,128,4096]{2,1,0:T(8,128)(2,1)}, bf16[1,128,512]{2,1,0:T(8,128)(2,1)}, bf16[1,128,512]{2,1,0:T(8,128)(2,1)}) custom-call(bf16[1,128,4096]{2,1,0:T(8,128)(2,1)S(1)} %get-tuple-element.8.refs_0_, bf16[1,128,4096]{2,1,0:T(8,128)(2,1)S(1)} %get-tuple-element.9.refs_1_, ...), custom_call_target="tpu_custom_call" | custom-call | tf_op jit(solution)/shard_map/pallas_call | solution.py:302
